TPU v7x, 32 devices: a whole 2x2x4 slice. The times are simulated.
32 devices in a mesh: dp: 4 (over y, x), sp: 4 (over z), shift: 2 (over core).
Axes of the slice: x: 2, y: 2, z: 4, core: 2. Of those that a mesh axis runs over, the one named last changes fastest.
Arguments:
- query_rows: bfloat16 [8, 1024, 32, 128], P(('shift', 'dp'), 'sp'), parts along dimension 0, may hold values from -6 to 6
- key_rows: bfloat16 [8, 1024, 32, 128], P(('shift', 'dp'), 'sp'), parts along dimension 0, may hold values from -6 to 6
- value_rows: bfloat16 [8, 1024, 32, 128], P(('shift', 'dp'), 'sp'), parts along dimension 0, may hold values from -6 to 6
- out_weight: bfloat16 [8192, 4096], P(('shift', 'dp')), parts along dimension 0, may hold values from -0.09375 to 0.09375
Outputs:
- mixer_out: bfloat16 [8, 1024, 4096], P(('shift', 'dp'), 'sp'), parts along dimension 0
There are 2 independent parts, one for each index of `shift`. A program takes and returns all parts, laid end to end along the dimension named above; each array names one. Nothing has to cross between parts.
All inputs are finite; a program needn't handle non-finite values.
Results may differ from a plain program's by a relative error of at most 0.006.
Values may be sent and summed in bfloat16 or wider, within the bound.
A program may use at most 128 MiB of HBM per device.

v0:
```python
import jax
import jax.numpy as jnp
from jax import lax
from jax.sharding import PartitionSpec as P


def feature_map(values):
    wide = values.astype(jnp.float32)
    return jnp.where(wide > 0.0, wide + 1.0, jnp.exp(jnp.minimum(wide, 0.0))).astype(jnp.bfloat16)


def plain_body(query_rows, key_rows, value_rows, out_weight):
    query_feature, key_feature = (feature_map(query_rows), feature_map(key_rows))
    count = query_rows.shape[1] * lax.axis_size("sp")
    state = (
        jnp.einsum("bthd,bthe->bhde", key_feature, value_rows, preferred_element_type=jnp.float32)
        / count
    )
    mass = jnp.sum(key_feature.astype(jnp.float32), axis=1) / count
    state = lax.psum(state.astype(jnp.bfloat16), "sp")
    mass = lax.psum(mass, "sp")
    top = jnp.einsum("bthd,bhde->bthe", query_feature, state, preferred_element_type=jnp.float32)
    bottom = jnp.einsum(
        "bthd,bhd->bth", query_feature.astype(jnp.float32), mass, precision=lax.Precision.HIGHEST
    )
    mixed = (top / (bottom + 0.001)[..., None] * count**0.5).astype(jnp.bfloat16)
    mixed = mixed.reshape(mixed.shape[0], mixed.shape[1], -1)
    mine = lax.all_to_all(mixed, "dp", split_axis=2, concat_axis=0, tiled=True)
    part = jnp.einsum("btw,wv->btv", mine, out_weight, preferred_element_type=jnp.float32)
    return lax.psum_scatter(part.astype(jnp.bfloat16), "dp", scatter_dimension=0, tiled=True)


def solution(mesh):
    placed = (
        P(("shift", "dp"), "sp", None, None),
        P(("shift", "dp"), "sp", None, None),
        P(("shift", "dp"), "sp", None, None),
        P(("shift", "dp"), None),
    )
    return jax.shard_map(
        plain_body,
        mesh=mesh,
        in_specs=placed,
        out_specs=P(("shift", "dp"), "sp", None),
        check_vma=False,
    )
```

profile of v0, /device:TPU:0, one launch (start us, length us, event | category | flops | bytes accessed | tf_op | source)
XLA Modules:
  0.0 271.4 jit_solution(5975725253797837042)
XLA Ops:
  6.5 0.0 copy-start
  6.5 0.0 all-reduce.3.cloned.1.call-start
  6.5 3.0 %convert_reduce_fusion = (f32[32,128]{1,0:T(8,128)S(1)}, bf16[256,32,128]{2,1,0:T(8,128)(2,1)S(1)}) fusion(bf16[1,256,32,128]{3,2,1,0:T(8,128)(2,1)} %param.5), kind=kLoop, calls=%fused_computation.18 | loop fusion | flops 8384512 | bytes 4210688 | tf_op jit(solution)/shard_map/reduce_sum | solution.py:19
  9.5 0.0 copy-done
  9.5 2.5 multiply_convert_fusion
  12.1 0.0 all-reduce.3.cloned.1.call-update
  12.1 0.0 reduce-scatter.4.cloned.1.call-start
  12.1 4.0 %fusion.13 = bf16[256,32,128]{2,1,0:T(8,128)(2,1)} fusion(bf16[1,256,32,128]{3,2,1,0:T(8,128)(2,1)} %param.4), kind=kLoop, calls=%fused_computation.19 | loop fusion | flops 6291456 | bytes 4194304 | tf_op jit(solution)/shard_map/reshape.5
  16.1 4.3 %copy.16 = bf16[256,32,128]{0,2,1:T(8,128)(2,1)} copy(bf16[256,32,128]{2,1,0:T(8,128)(2,1)} %fusion.13) | data formatting | bytes 4194304 | tf_op jit(solution)/shard_map/reshape.5
  20.4 21.4 %psum.15 = f32[32,128]{1,0:T(8,128)S(1)} all-reduce(f32[32,128]{1,0:T(8,128)S(1)} %broadcast_multiply_fusion), channel_id=1, replica_groups=mesh['dp'=4,'sp'=4,'shift'=2] {'sp'}, use_global_device_ids=true, to_apply=%region_2.3 | all-reduce | flops 4096 | bytes 32768 | tf_op jit(solution)/shard_map/psum | solution.py:21
  41.8 2.5 fusion.24
  44.3 23.1 %all-reduce.3.cloned.1.call-done = bf16[32,128,128]{2,1,0:T(8,128)(2,1)} async-done(((bf16[32,128,128]{2,1,0:T(8,128)(2,1)}), bf16[32,128,128]{2,1,0:T(8,128)(2,1)}) %all-reduce.3.cloned.1.call-update) | async-done | bytes 1048592 | tf_op jit(solution)/shard_map/psum | solution.py:20
  67.4 2.7 fusion.12
  70.1 25.1 %copy.29 = bf16[1,256,4096]{1,0,2:T(2,128)(2,1)} copy(bf16[1,256,4096]{1,2,0:T(8,128)(2,1)S(1)} %bitcast.51) | data formatting | bytes 4194304 | tf_op jit(solution)/shard_map/reshape | solution.py:27
  95.1 0.5 broadcast.38
  95.6 22.9 %reduce.1 = bf16[4096,256]{1,0:T(8,128)(2,1)} reduce(bf16[4096,1,256]{2,1,0:T(2,128)(2,1)} %bitcast.48, bf16[]{:T(256)} %broadcast.38), dimensions={1}, to_apply=%bitcast.46.reduce_sub_computation | reduce | bytes 4194306
  118.5 4.0 %reshape.52 = bf16[4,2,131072]{2,1,0:T(2,128)(2,1)} reshape(bf16[4096,256]{1,0:T(8,128)(2,1)} %reduce.1) | data formatting | bytes 4194304
  122.5 30.2 %all_to_all.18 = bf16[4,2,131072]{2,1,0:T(2,128)(2,1)} all-to-all(bf16[4,2,131072]{2,1,0:T(2,128)(2,1)} %reshape.52), channel_id=1, replica_groups=mesh['dp'=4,'sp'=4,'shift'=2] {'dp'}, dimensions={0} | all-to-all | bytes 4194304 | tf_op jit(solution)/shard_map/all_to_all | solution.py:28
  152.7 5.0 %reshape.53 = bf16[4096,1,256]{2,1,0:T(2,128)(2,1)} reshape(bf16[4,2,131072]{2,1,0:T(2,128)(2,1)} %all_to_all.18) | data formatting | bytes 4194304
  157.7 3.9 %copy.18 = bf16[1,256,4096]{1,2,0:T(8,128)(2,1)} copy(bf16[1,256,4096]{1,0,2:T(2,128)(2,1)} %bitcast.49) | data formatting | bytes 4194304
  161.6 4.0 %copy.13 = bf16[1,256,4,1024]{3,1,2,0:T(8,128)(2,1)} copy(bf16[1,256,4,1024]{1,3,2,0:T(8,128)(2,1)} %bitcast.50) | data formatting | bytes 4194304 | tf_op jit(solution)/shard_map/all_to_all | solution.py:28
  165.5 14.7 %fusion.2 = bf16[4,256,4096]{2,1,0:T(8,128)(2,1)} fusion(bf16[1024,4096]{1,0:T(8,128)(2,1)} %param.7, bf16[1,256,4,1024]{3,1,2,0:T(8,128)(2,1)} %copy.13), kind=kOutput, calls=%fused_computation.2 | convolution fusion | flops 8594128896 | bytes 18874368 | tf_op jit(solution)/shard_map/btw,wv->btv/dot_general | solution.py:29
  180.2 0.0 reduce-scatter.4.cloned.1.call-update
  180.3 84.3 %reduce-scatter.4.cloned.1.call-done = bf16[1,256,4096]{2,1,0:T(8,128)(2,1)} async-done(((bf16[4,256,4096]{2,1,0:T(8,128)(2,1)}), bf16[1,256,4096]{2,1,0:T(8,128)(2,1)}) %reduce-scatter.4.cloned.1.call-update) | async-done | bytes 2097168
  (2 shorter events, 0.0 us)
Async XLA Ops:
  6.5 3.0 %copy-start = (bf16[1,256,32,128]{3,2,1,0:T(8,128)(2,1)S(1)}, bf16[1,256,32,128]{3,2,1,0:T(8,128)(2,1)}, u32[]{:S(2)}) copy-start(bf16[1,256,32,128]{3,2,1,0:T(8,128)(2,1)} %param.6) | copy-start | bytes 6291460
  6.5 60.8 %all-reduce.3.cloned.1.call-start = ((), (), s32[]{:S(2)}) async-start(), calls=%async_computation.2 | async-start | bytes 2097152 | tf_op jit(solution)/shard_map/psum | solution.py:20
  12.1 252.4 %reduce-scatter.4.cloned.1.call-start = ((), (), s32[]{:S(2)}) async-start(), calls=%async_computation.3 | async-start | bytes 10485760
Sparse Core Ops, SparseCore 0:
  12.2 55.1 all-reduce.2
  180.4 84.0 reduce-scatter.3
where the time goes:
time: 272 us; the launch traced here: 271 us
  waiting for transfers between devices  107 us (39%)
  blocking collectives  51.6 us (19%)
  local copies, waits for them, and re-layouts  46.7 us (17%)
  other arithmetic  29.8 us (11%)
  matrix products  22.4 us (8%)
  between operations  13.4 us (5%)
    unnamed x3, waiting for transfers between devices  84.3 us
    all_to_all x1, blocking collectives, plain_body(): mine = lax.all_to_all(mixed, 'dp', split_axis=2, concat_axis=0, tiled=True)  30.2 us
    reshape x1, local copies, waits for them, and re-layouts, plain_body(): mixed = mixed.reshape(mixed.shape[0], mixed.shape[1], -1)  25.1 us
    psum x1, waiting for transfers between devices, plain_body(): state = lax.psum(state.astype(jnp.bfloat16), 'sp')  23.1 us
    unnamed x1, other arithmetic  22.9 us
    psum x1, blocking collectives, plain_body(): mass = lax.psum(mass, 'sp')  21.4 us
    dot_general x1, matrix products, plain_body(): jnp.einsum('btw,wv->btv', mine, out_weight, preferred_element_type=jnp.fl...  14.7 us
    unnamed x6, local copies, waits for them, and re-layouts  13.4 us
  transfers between devices with their start and end apart: 2, of which 2 were waited for; matrix products, arithmetic and copies ran while one was open for 4% of the time, Pallas kernels for 0%

commit v1 on v0

--- a/solution.py
+++ b/solution.py
@@ -25,7 +25,10 @@
     )
     mixed = (top / (bottom + 0.001)[..., None] * count**0.5).astype(jnp.bfloat16)
     mixed = mixed.reshape(mixed.shape[0], mixed.shape[1], -1)
-    mine = lax.all_to_all(mixed, "dp", split_axis=2, concat_axis=0, tiled=True)
+    size = lax.axis_size("dp")
+    parts = jnp.stack(jnp.split(mixed, size, axis=2), axis=0)
+    parts = lax.all_to_all(parts, "dp", split_axis=0, concat_axis=0)
+    mine = jnp.concatenate(parts, axis=0)
     part = jnp.einsum("btw,wv->btv", mine, out_weight, preferred_element_type=jnp.float32)
     return lax.psum_scatter(part.astype(jnp.bfloat16), "dp", scatter_dimension=0, tiled=True)
 

time: 272 us -> 214 us (0.79)
  local copies, waits for them, and re-layouts: 46.7 us -> 11.8 us
  other arithmetic: 29.8 us -> 8.58 us
    reshape x1 -> x0, local copies, waits for them, and re-layouts: 25.1 us -> none  [plain_body(): mixed = mixed.reshape(mixed.shape[0], mixed.shape[1], -1)]
    unnamed x1 -> x0, other arithmetic: 22.9 us -> none
    unnamed x6, local copies, waits for them, and re-layouts: 13.4 us -> 6.37 us
    all_to_all x1 -> x0, local copies, waits for them, and re-layouts: 3.97 us -> none  [plain_body(): mine = lax.all_to_all(mixed, 'dp', split_axis=2, concat_axis=0, tiled=True)]
    another operation x1 -> x2, other arithmetic: 4 us -> 5.61 us
  transfers between devices with their start and end apart: 2 -> 2, of which waited for: 2 -> 2; matrix products, arithmetic and copies ran while one was open for 4% -> 5% of each run, Pallas kernels for 0% -> 0%
where the time goes in v1:
time: 214 us
  waiting for transfers between devices  107 us (50%)
  blocking collectives  50.3 us (24%)
  matrix products  22 us (10%)
  between operations  13.4 us (6%)
  local copies, waits for them, and re-layouts  11.8 us (6%)
  other arithmetic  8.58 us (4%)
    unnamed x3, waiting for transfers between devices  84.3 us
    all_to_all x1, blocking collectives, plain_body(): parts = lax.all_to_all(parts, 'dp', split_axis=0, concat_axis=0)  28.9 us
    psum x1, waiting for transfers between devices, plain_body(): state = lax.psum(state.astype(jnp.bfloat16), 'sp')  23.1 us
    psum x1, blocking collectives, plain_body(): mass = lax.psum(mass, 'sp')  21.4 us
    dot_general x1, matrix products, plain_body(): jnp.einsum('btw,wv->btv', mine, out_weight, preferred_element_type=jnp.fl...  14.3 us
    unnamed x6, local copies, waits for them, and re-layouts  6.37 us
  transfers between devices with their start and end apart: 2, of which 2 were waited for; matrix products, arithmetic and copies ran while one was open for 5% of the time, Pallas kernels for 0%

profile of v1, /device:TPU:0, one launch (start us, length us, event | category | flops | bytes accessed | tf_op | source)
XLA Modules:
  0.0 213.5 jit_solution(17224997726878175967)
XLA Ops:
  6.5 0.0 copy-start
  6.5 0.0 all-reduce.3.cloned.1.call-start
  6.5 3.0 %convert_reduce_fusion = (f32[32,128]{1,0:T(8,128)S(1)}, bf16[256,32,128]{2,1,0:T(8,128)(2,1)S(1)}) fusion(bf16[1,256,32,128]{3,2,1,0:T(8,128)(2,1)} %param.5), kind=kLoop, calls=%fused_computation.18 | loop fusion | flops 8384512 | bytes 4210688 | tf_op jit(solution)/shard_map/reduce_sum | solution.py:19
  9.5 0.0 copy-done
  9.5 2.5 %multiply_convert_fusion = bf16[32,128,128]{1,2,0:T(8,128)(2,1)} fusion(bf16[256,32,128]{2,1,0:T(8,128)(2,1)S(1)} %bitcast.44, bf16[256,32,128]{2,1,0:T(8,128)(2,1)S(1)} %get-tuple-element.10), kind=kOutput, calls=%fused_computation.25 | convolution fusion | flops 269484032 | bytes 5242880 | tf_op jit(solution)/shard_map/bthd,bthe->bhde/dot_general | solution.py:16
  12.1 0.0 all-reduce.3.cloned.1.call-update
  12.1 0.0 reduce-scatter.4.cloned.1.call-start
  12.1 4.0 %fusion.13 = bf16[256,32,128]{2,1,0:T(8,128)(2,1)} fusion(bf16[1,256,32,128]{3,2,1,0:T(8,128)(2,1)} %param.4), kind=kLoop, calls=%fused_computation.19 | loop fusion | flops 6291456 | bytes 4194304 | tf_op jit(solution)/shard_map/reshape.6
  16.1 4.3 %copy.18 = bf16[256,32,128]{0,2,1:T(8,128)(2,1)} copy(bf16[256,32,128]{2,1,0:T(8,128)(2,1)} %fusion.13) | data formatting | bytes 4194304 | tf_op jit(solution)/shard_map/reshape.6
  20.4 21.4 %psum.15 = f32[32,128]{1,0:T(8,128)S(1)} all-reduce(f32[32,128]{1,0:T(8,128)S(1)} %broadcast_multiply_fusion), channel_id=1, replica_groups=mesh['dp'=4,'sp'=4,'shift'=2] {'sp'}, use_global_device_ids=true, to_apply=%region_2.3 | all-reduce | flops 4096 | bytes 32768 | tf_op jit(solution)/shard_map/psum | solution.py:21
  41.8 2.5 %fusion.25 = f32[32,1,256]{2,1,0:T(1,128)S(1)} fusion(f32[32,128,1]{1,2,0:T(1,128)S(1)} %bitcast.50, bf16[256,32,128]{0,2,1:T(8,128)(2,1)} %copy.18), kind=kOutput, calls=%fused_computation.31 | convolution fusion | flops 12582912 | bytes 2146304 | tf_op jit(solution)/shard_map/bthd,bhd->bth/dot_general | solution.py:23
  44.3 23.1 %all-reduce.3.cloned.1.call-done = bf16[32,128,128]{1,2,0:T(8,128)(2,1)} async-done(((bf16[32,128,128]{1,2,0:T(8,128)(2,1)}), bf16[32,128,128]{1,2,0:T(8,128)(2,1)}) %all-reduce.3.cloned.1.call-update) | async-done | bytes 1048592 | tf_op jit(solution)/shard_map/psum | solution.py:20
  67.4 2.6 %fusion.12 = bf16[1,256,32,128]{1,3,2,0:T(8,128)(2,1)S(1)} fusion(bf16[32,128,128]{1,2,0:T(8,128)(2,1)} %all-reduce.3.cloned.1.call-done, bf16[256,32,128]{0,2,1:T(8,128)(2,1)} %copy.18, f32[256,32]{0,1:T(8,128)S(1)} %fusion.23), kind=kOutput, calls=%fused_computation.17 | convolution fusion | flops 271581184 | bytes 5275648 | tf_op jit(solution)/shard_map/bthd,bhde->bthe/dot_general | solution.py:22
  70.0 1.2 fusion.24
  71.2 1.2 copy.20
  72.4 2.1 copy.22
  74.5 2.1 copy.21
  76.5 1.0 copy.23
  77.5 1.6 pad_maximum_fusion
  79.2 28.9 %all_to_all.5 = bf16[4,1,256,1024]{3,2,1,0:T(8,128)(2,1)S(1)} all-to-all(bf16[4,1,256,1024]{3,2,1,0:T(8,128)(2,1)S(1)} %pad_maximum_fusion), channel_id=1, replica_groups=mesh['dp'=4,'sp'=4,'shift'=2] {'dp'}, dimensions={0} | all-to-all | bytes 4194304 | tf_op jit(solution)/shard_map/all_to_all | solution.py:30
  108.1 14.3 %fusion.2 = bf16[4,256,4096]{2,1,0:T(8,128)(2,1)} fusion(bf16[1024,4096]{1,0:T(8,128)(2,1)} %param.7, bf16[4,1,256,1024]{3,2,1,0:T(8,128)(2,1)S(1)} %all_to_all.5), kind=kOutput, calls=%fused_computation.2 | convolution fusion | flops 8594128896 | bytes 18874368 | tf_op jit(solution)/shard_map/btw,wv->btv/dot_general | solution.py:32
  122.4 0.0 reduce-scatter.4.cloned.1.call-update
  122.5 84.2 %reduce-scatter.4.cloned.1.call-done = bf16[1,256,4096]{2,1,0:T(8,128)(2,1)} async-done(((bf16[4,256,4096]{2,1,0:T(8,128)(2,1)}), bf16[1,256,4096]{2,1,0:T(8,128)(2,1)}) %reduce-scatter.4.cloned.1.call-update) | async-done | bytes 2097168
  (2 shorter events, 0.0 us)
Async XLA Ops:
  6.5 3.0 %copy-start = (bf16[1,256,32,128]{3,2,1,0:T(8,128)(2,1)S(1)}, bf16[1,256,32,128]{3,2,1,0:T(8,128)(2,1)}, u32[]{:S(2)}) copy-start(bf16[1,256,32,128]{3,2,1,0:T(8,128)(2,1)} %param.6) | copy-start | bytes 6291460
  6.5 60.8 %all-reduce.3.cloned.1.call-start = ((), (), s32[]{:S(2)}) async-start(), calls=%async_computation.2 | async-start | bytes 2097152 | tf_op jit(solution)/shard_map/psum | solution.py:20
  12.1 194.6 %reduce-scatter.4.cloned.1.call-start = ((), (), s32[]{:S(2)}) async-start(), calls=%async_computation.3 | async-start | bytes 10485760
Sparse Core Ops, SparseCore 0:
  12.2 55.1 all-reduce.2
  122.6 84.0 reduce-scatter.3
